TPU v7x, 32 devices: a whole 2x2x4 slice. The times are simulated.
32 devices in a mesh: group: 4 (over y, x), replica: 8 (over z, core).
Axes of the slice: x: 2, y: 2, z: 4, core: 2. Of those that a mesh axis runs over, the one named last changes fastest.
Arguments:
- inputs: bfloat16 [4096, 2048], P(('group', 'replica')), may hold values from -6 to 6
- cotangent: bfloat16 [4096, 2048], P(('group', 'replica')), may hold values from -6 to 6
- block_map: int32 [4, 8], P('group'), may hold values from 0 to 7, as said below
- positions: int32 [4096], P(('group', 'replica')), may hold values from 0 to 1023, as said below
- step_count: int32 [1], replicated, may hold values from 1 to 20
- weight_qkv: float32 [2048, 4096], P(('group', 'replica')), may hold values from -0.125 to 0.125
- first_qkv: float32 [2048, 4096], P(('group', 'replica')), may hold values from -6 to 6
- second_qkv: float32 [2048, 4096], P(('group', 'replica')), may hold values from 64 to 1024
- weight_out: float32 [2048, 2048], P(('group', 'replica')), may hold values from -1.5 to 1.5
- first_out: float32 [2048, 2048], P(('group', 'replica')), may hold values from -6 to 6
- second_out: float32 [2048, 2048], P(('group', 'replica')), may hold values from 0.5 to 5
- weight_gate_up: float32 [2048, 12288], P(('group', 'replica')), may hold values from -0.125 to 0.125
- first_gate_up: float32 [2048, 12288], P(('group', 'replica')), may hold values from -6 to 6
- second_gate_up: float32 [2048, 12288], P(('group', 'replica')), may hold values from 0.5 to 5
- weight_down: float32 [6144, 2048], P(('group', 'replica')), may hold values from -0.078125 to 0.078125
- first_down: float32 [6144, 2048], P(('group', 'replica')), may hold values from -6 to 6
- second_down: float32 [6144, 2048], P(('group', 'replica')), may hold values from 0.5 to 5
- norm_gains: float32 [4352], P(('group', 'replica')), may hold values from 0.5 to 1.5
- first_gains: float32 [4352], P(('group', 'replica')), may hold values from -6 to 6
- second_gains: float32 [4352], P(('group', 'replica')), may hold values from 64 to 1024
Outputs:
- block_out: bfloat16 [4096, 2048], P(('group', 'replica'))
- input_grad: float32 [4096, 2048], P(('group', 'replica'))
- grad_qkv: float32 [2048, 4096], P(('group', 'replica'))
- grad_out: float32 [2048, 2048], P(('group', 'replica'))
- grad_gate_up: float32 [2048, 12288], P(('group', 'replica'))
- grad_down: float32 [6144, 2048], P(('group', 'replica'))
- grad_gains: float32 [4352], P(('group', 'replica'))
- new_qkv: float32 [2048, 4096], P(('group', 'replica'))
- new_first_qkv: float32 [2048, 4096], P(('group', 'replica'))
- new_second_qkv: float32 [2048, 4096], P(('group', 'replica'))
- new_out: float32 [2048, 2048], P(('group', 'replica'))
- new_first_out: float32 [2048, 2048], P(('group', 'replica'))
- new_second_out: float32 [2048, 2048], P(('group', 'replica'))
- new_gate_up: float32 [2048, 12288], P(('group', 'replica'))
- new_first_gate_up: float32 [2048, 12288], P(('group', 'replica'))
- new_second_gate_up: float32 [2048, 12288], P(('group', 'replica'))
- new_down: float32 [6144, 2048], P(('group', 'replica'))
- new_first_down: float32 [6144, 2048], P(('group', 'replica'))
- new_second_down: float32 [6144, 2048], P(('group', 'replica'))
- new_gains: float32 [4352], P(('group', 'replica'))
- new_first_gains: float32 [4352], P(('group', 'replica'))
- new_second_gains: float32 [4352], P(('group', 'replica'))
Inputs may be any that keep to these rules, and one draw needn't show every extreme that they name: Each row is a permutation: slot s of group g holds tokens block_map[g, s] * 128 to block_map[g, s] * 128 + 127 of the group's 1 sequence laid end to end. Within each sequence, in token order, positions count up from 0 and restart at 0 at most once; some sequence has no restart.
All inputs are finite; a program needn't handle non-finite values.
Results may differ from a plain program's by a relative error of at most 0.04.
The roundings to bfloat16 on the way count: a program that leaves them out, or rounds other values in their place, can miss the bound.
Values may be sent and summed in bfloat16 or wider, within the bound.
A program may use at most 576 MiB of HBM per device.

v0:
```python
import jax
import jax.numpy as jnp
from jax import lax
from jax.sharding import PartitionSpec as P

D = 2048
H = 16
KVH = 8
HD = 128
FF = 6144
C = 128
SPG = 1


norm_eps = 1e-06
rope_base = 1000000.0
learn_rate = 0.1
beta_first = 0.9
beta_second = 0.95
adam_eps = 1e-08
decay_rate = 0.1
masked_score = -1e30


def rms_scale(values):
    return lax.rsqrt(jnp.mean(values * values, axis=-1, keepdims=True) + norm_eps)


def norm_back(grad_normed, normed, scale):
    return scale * (grad_normed - normed * jnp.mean(grad_normed * normed, axis=-1, keepdims=True))


def rope_tables(token_pos):
    half_dim = HD // 2
    frequency = rope_base ** (-(jnp.arange(half_dim).astype(jnp.float32) * 2.0 / HD))
    angles = token_pos.astype(jnp.float32)[:, None] * frequency[None, :]
    return (jnp.cos(angles)[:, None, :], jnp.sin(angles)[:, None, :])


def rotate(vectors, cosine, sine_table):
    half_dim = vectors.shape[-1] // 2
    first_half = vectors[..., :half_dim]
    second_half = vectors[..., half_dim:]
    return jnp.concatenate(
        [
            first_half * cosine - second_half * sine_table,
            second_half * cosine + first_half * sine_table,
        ],
        axis=-1,
    )


def unrotate(gradients, cosine, sine_table):
    half_dim = gradients.shape[-1] // 2
    first_half = gradients[..., :half_dim]
    second_half = gradients[..., half_dim:]
    return jnp.concatenate(
        [
            first_half * cosine + second_half * sine_table,
            second_half * cosine - first_half * sine_table,
        ],
        axis=-1,
    )


def key_ordinals(map_row, offset, row_count):
    row_ids = offset + jnp.arange(row_count, dtype=jnp.int32)
    slot_ids = row_ids // C
    matches = slot_ids[:, None] == jnp.arange(map_row.shape[0], dtype=jnp.int32)[None, :]
    return jnp.sum(jnp.where(matches, map_row[None, :], 0), axis=1) * C + row_ids % C


def visible(query_ord, key_ord, seq_len):
    same_sequence = key_ord[None, :] // seq_len == query_ord[:, None] // seq_len
    return same_sequence & (key_ord[None, :] <= query_ord[:, None])


def adam_step(weight, first_moment, second, gradient, step_value, decay_value):
    new_first = beta_first * first_moment + (1.0 - beta_first) * gradient
    new_second = beta_second * second + (1.0 - beta_second) * gradient * gradient
    first_hat = new_first / (1.0 - beta_first**step_value)
    second_hat = new_second / (1.0 - beta_second**step_value)
    new_weight = weight - learn_rate * (
        first_hat / (jnp.sqrt(second_hat) + adam_eps) + decay_value * weight
    )
    return (new_weight, new_first, new_second)


def local(
    inputs,
    cotangent,
    block_map,
    positions,
    step_count,
    weight_qkv,
    first_qkv,
    second_qkv,
    weight_out,
    first_out,
    second_out,
    weight_gate_up,
    first_gate_up,
    second_gate_up,
    weight_down,
    first_down,
    second_down,
    norm_gains,
    first_gains,
    second_gains,
):
    tok_rows = inputs.shape[0]
    head_ratio = H // KVH
    attn_scale = HD ** (-0.5)
    map_row = block_map[0]
    seq_len = map_row.shape[0] * C // SPG
    query_ord = key_ordinals(map_row, lax.axis_index("replica") * tok_rows, tok_rows)
    qkv_full, out_full, gains_full = (
        lax.all_gather(weight_qkv.astype(jnp.bfloat16), ("group", "replica"), axis=0, tiled=True),
        lax.all_gather(weight_out.astype(jnp.bfloat16), ("group", "replica"), axis=0, tiled=True),
        lax.all_gather(norm_gains.astype(jnp.bfloat16), ("group", "replica"), axis=0, tiled=True),
    )
    gain_values = gains_full.astype(jnp.float32)
    gain_one = gain_values[:D]
    gain_two = gain_values[D : 2 * D]
    gain_query = gain_values[2 * D : 2 * D + HD]
    gain_key = gain_values[2 * D + HD :]
    inputs_f = inputs.astype(jnp.float32)
    scale_one = rms_scale(inputs_f)
    normed_one = inputs_f * scale_one
    hidden_one = (normed_one * gain_one).astype(jnp.bfloat16)
    projected = jnp.dot(hidden_one, qkv_full, preferred_element_type=jnp.float32)
    query_raw = projected[:, : H * HD].reshape(tok_rows, H, HD)
    key_raw = projected[:, H * HD : (H + KVH) * HD].reshape(tok_rows, KVH, HD)
    value_rows = projected[:, (H + KVH) * HD :].reshape(tok_rows, KVH, HD).astype(jnp.bfloat16)
    cosine, sine_table = rope_tables(positions)
    query_scale = rms_scale(query_raw)
    query_hat = query_raw * query_scale
    key_scale = rms_scale(key_raw)
    key_hat = key_raw * key_scale
    query_rot = (rotate(query_hat * gain_query, cosine, sine_table) * attn_scale).astype(
        jnp.bfloat16
    )
    key_rot = rotate(key_hat * gain_key, cosine, sine_table).astype(jnp.bfloat16)
    query_groups = query_rot.reshape(tok_rows, KVH, head_ratio, HD)
    run_max = jnp.full((KVH, head_ratio, tok_rows), masked_score, jnp.float32)
    key_piece = lax.all_gather(key_rot, "replica", axis=0, tiled=True)
    value_piece = lax.all_gather(value_rows, "replica", axis=0, tiled=True)
    allowed = visible(query_ord, key_ordinals(map_row, jnp.int32(0), key_piece.shape[0]), seq_len)
    scores = jnp.einsum(
        "qgrd,kgd->grqk", query_groups, key_piece, preferred_element_type=jnp.float32
    )
    scores = jnp.where(allowed, scores, masked_score)
    new_max = jnp.maximum(run_max, jnp.max(scores, axis=-1))
    attn_probs = jnp.where(allowed, jnp.exp(scores - new_max[..., None]), 0.0)
    new_sum = jnp.sum(attn_probs, axis=-1)
    mixed_part = jnp.einsum(
        "grqk,kgd->grqd",
        attn_probs.astype(jnp.bfloat16),
        value_piece,
        preferred_element_type=jnp.float32,
    )
    log_total = new_max + jnp.log(new_sum)
    mixed_rows = (
        (mixed_part / new_sum[..., None])
        .transpose(2, 0, 1, 3)
        .reshape(tok_rows, H * HD)
        .astype(jnp.bfloat16)
    )
    resid_one = inputs_f + jnp.dot(mixed_rows, out_full, preferred_element_type=jnp.float32)
    scale_two = rms_scale(resid_one)
    normed_two = resid_one * scale_two
    hidden_two = (normed_two * gain_two).astype(jnp.bfloat16)
    gu_full, down_full = (
        lax.all_gather(
            weight_gate_up.astype(jnp.bfloat16), ("group", "replica"), axis=0, tiled=True
        ),
        lax.all_gather(weight_down.astype(jnp.bfloat16), ("group", "replica"), axis=0, tiled=True),
    )
    gate_up = jnp.dot(hidden_two, gu_full, preferred_element_type=jnp.float32)
    gate_in = gate_up[:, :FF]
    up_in = gate_up[:, FF:]
    sigmoid_gate = jax.nn.sigmoid(gate_in)
    silu_gate = gate_in * sigmoid_gate
    activated = (silu_gate * up_in).astype(jnp.bfloat16)
    block_out = (
        resid_one + jnp.dot(activated, down_full, preferred_element_type=jnp.float32)
    ).astype(jnp.bfloat16)
    act_grad = jnp.dot(cotangent, down_full.T, preferred_element_type=jnp.float32)
    gate_grad = act_grad * up_in * sigmoid_gate * (1.0 + gate_in * (1.0 - sigmoid_gate))
    up_grad = act_grad * silu_gate
    gate_up_grad = jnp.concatenate([gate_grad, up_grad], axis=1).astype(jnp.bfloat16)
    hidden_two_grad = jnp.dot(gate_up_grad, gu_full.T, preferred_element_type=jnp.float32)
    grad_down_part = jnp.dot(activated.T, cotangent, preferred_element_type=jnp.float32)
    grad_gate_up_part = jnp.dot(hidden_two.T, gate_up_grad, preferred_element_type=jnp.float32)
    gain_two_grad = jnp.sum(hidden_two_grad * normed_two, axis=0)
    resid_grad = cotangent.astype(jnp.float32) + norm_back(
        hidden_two_grad * gain_two, normed_two, scale_two
    )
    mlp_shares = (
        lax.psum_scatter(
            grad_gate_up_part.astype(jnp.bfloat16), "group", scatter_dimension=0, tiled=True
        ).astype(jnp.float32),
        lax.psum_scatter(
            grad_down_part.astype(jnp.bfloat16), "group", scatter_dimension=0, tiled=True
        ).astype(jnp.float32),
    )
    attn_grad = resid_grad.astype(jnp.bfloat16)
    grad_out_part = jnp.dot(mixed_rows.T, attn_grad, preferred_element_type=jnp.float32)
    mixed_grad = jnp.dot(attn_grad, out_full.T, preferred_element_type=jnp.float32).astype(
        jnp.bfloat16
    )
    mixed_grad_groups = mixed_grad.reshape(tok_rows, KVH, head_ratio, HD).transpose(1, 2, 0, 3)
    row_delta = jnp.sum(
        mixed_grad.astype(jnp.float32).reshape(tok_rows, KVH, head_ratio, HD)
        * mixed_rows.astype(jnp.float32).reshape(tok_rows, KVH, head_ratio, HD),
        axis=-1,
    ).transpose(1, 2, 0)
    key_piece = lax.all_gather(key_rot, "replica", axis=0, tiled=True)
    value_piece = lax.all_gather(value_rows, "replica", axis=0, tiled=True)
    row_count = key_piece.shape[0]
    allowed = visible(query_ord, key_ordinals(map_row, jnp.int32(0), row_count), seq_len)
    scores = jnp.einsum(
        "qgrd,kgd->grqk", query_groups, key_piece, preferred_element_type=jnp.float32
    )
    attn_probs = jnp.where(allowed, jnp.exp(scores - log_total[..., None]), 0.0)
    value_grad = jnp.einsum(
        "grqk,grqd->kgd",
        attn_probs.astype(jnp.bfloat16),
        mixed_grad_groups,
        preferred_element_type=jnp.float32,
    )
    prob_grad = jnp.einsum(
        "grqd,kgd->grqk", mixed_grad_groups, value_piece, preferred_element_type=jnp.float32
    )
    score_grad = (attn_probs * (prob_grad - row_delta[..., None])).astype(jnp.bfloat16)
    query_grad = jnp.einsum(
        "grqk,kgd->grqd", score_grad, key_piece, preferred_element_type=jnp.float32
    )
    key_grad = jnp.einsum(
        "grqk,qgrd->kgd", score_grad, query_groups, preferred_element_type=jnp.float32
    )
    rows_grad = jnp.stack([key_grad, value_grad], axis=1).reshape(row_count, 2, KVH * HD)
    query_grad, key_value_grad = (query_grad, rows_grad)
    own_grads = lax.psum_scatter(
        key_value_grad.astype(jnp.bfloat16), "replica", scatter_dimension=0, tiled=True
    ).astype(jnp.float32)
    key_grad_rows = own_grads[:, 0].reshape(tok_rows, KVH, HD)
    value_grad_rows = own_grads[:, 1]
    query_grad_rows = query_grad.transpose(2, 0, 1, 3).reshape(tok_rows, H, HD)
    query_norm_grad = unrotate(query_grad_rows * attn_scale, cosine, sine_table)
    gain_query_grad = jnp.sum(query_norm_grad * query_hat, axis=(0, 1))
    query_raw_grad = norm_back(query_norm_grad * gain_query, query_hat, query_scale)
    key_norm_grad = unrotate(key_grad_rows, cosine, sine_table)
    gain_key_grad = jnp.sum(key_norm_grad * key_hat, axis=(0, 1))
    key_raw_grad = norm_back(key_norm_grad * gain_key, key_hat, key_scale)
    projected_grad = jnp.concatenate(
        [
            query_raw_grad.reshape(tok_rows, H * HD),
            key_raw_grad.reshape(tok_rows, KVH * HD),
            value_grad_rows,
        ],
        axis=1,
    ).astype(jnp.bfloat16)
    grad_qkv_part = jnp.dot(hidden_one.T, projected_grad, preferred_element_type=jnp.float32)
    hidden_one_grad = jnp.dot(projected_grad, qkv_full.T, preferred_element_type=jnp.float32)
    gain_one_grad = jnp.sum(hidden_one_grad * normed_one, axis=0)
    input_grad = resid_grad + norm_back(hidden_one_grad * gain_one, normed_one, scale_one)
    grad_gains_part = jnp.concatenate(
        [gain_one_grad, gain_two_grad, gain_query_grad, gain_key_grad]
    )
    attn_shares = (
        lax.psum_scatter(
            grad_qkv_part.astype(jnp.bfloat16), "group", scatter_dimension=0, tiled=True
        ).astype(jnp.float32),
        lax.psum_scatter(
            grad_out_part.astype(jnp.bfloat16), "group", scatter_dimension=0, tiled=True
        ).astype(jnp.float32),
        lax.psum_scatter(
            grad_gains_part.astype(jnp.bfloat16), "group", scatter_dimension=0, tiled=True
        ).astype(jnp.float32),
    )
    grad_qkv, grad_out, grad_gains, grad_gate_up, grad_down = (
        lax.psum_scatter(
            attn_shares[0].astype(jnp.bfloat16), "replica", scatter_dimension=0, tiled=True
        ).astype(jnp.float32),
        lax.psum_scatter(
            attn_shares[1].astype(jnp.bfloat16), "replica", scatter_dimension=0, tiled=True
        ).astype(jnp.float32),
        lax.psum_scatter(
            attn_shares[2].astype(jnp.bfloat16), "replica", scatter_dimension=0, tiled=True
        ).astype(jnp.float32),
        lax.psum_scatter(
            mlp_shares[0].astype(jnp.bfloat16), "replica", scatter_dimension=0, tiled=True
        ).astype(jnp.float32),
        lax.psum_scatter(
            mlp_shares[1].astype(jnp.bfloat16), "replica", scatter_dimension=0, tiled=True
        ).astype(jnp.float32),
    )
    step_value = step_count[0].astype(jnp.float32)
    new_qkv, new_first_qkv, new_second_qkv = adam_step(
        weight_qkv, first_qkv, second_qkv, grad_qkv, step_value, decay_rate
    )
    new_out, new_first_out, new_second_out = adam_step(
        weight_out, first_out, second_out, grad_out, step_value, decay_rate
    )
    new_gate_up, new_first_gate_up, new_second_gate_up = adam_step(
        weight_gate_up, first_gate_up, second_gate_up, grad_gate_up, step_value, decay_rate
    )
    new_down, new_first_down, new_second_down = adam_step(
        weight_down, first_down, second_down, grad_down, step_value, decay_rate
    )
    new_gains, new_first_gains, new_second_gains = adam_step(
        norm_gains, first_gains, second_gains, grad_gains, step_value, 0.0
    )
    return (
        block_out,
        input_grad,
        grad_qkv,
        grad_out,
        grad_gate_up,
        grad_down,
        grad_gains,
        new_qkv,
        new_first_qkv,
        new_second_qkv,
        new_out,
        new_first_out,
        new_second_out,
        new_gate_up,
        new_first_gate_up,
        new_second_gate_up,
        new_down,
        new_first_down,
        new_second_down,
        new_gains,
        new_first_gains,
        new_second_gains,
    )


def solution(mesh):
    in_specs = (
        P(("group", "replica"), None),
        P(("group", "replica"), None),
        P("group", None),
        P(("group", "replica")),
        P(),
        P(("group", "replica"), None),
        P(("group", "replica"), None),
        P(("group", "replica"), None),
        P(("group", "replica"), None),
        P(("group", "replica"), None),
        P(("group", "replica"), None),
        P(("group", "replica"), None),
        P(("group", "replica"), None),
        P(("group", "replica"), None),
        P(("group", "replica"), None),
        P(("group", "replica"), None),
        P(("group", "replica"), None),
        P(("group", "replica")),
        P(("group", "replica")),
        P(("group", "replica")),
    )
    out_specs = (
        P(("group", "replica"), None),
        P(("group", "replica"), None),
        P(("group", "replica"), None),
        P(("group", "replica"), None),
        P(("group", "replica"), None),
        P(("group", "replica"), None),
        P(("group", "replica")),
        P(("group", "replica"), None),
        P(("group", "replica"), None),
        P(("group", "replica"), None),
        P(("group", "replica"), None),
        P(("group", "replica"), None),
        P(("group", "replica"), None),
        P(("group", "replica"), None),
        P(("group", "replica"), None),
        P(("group", "replica"), None),
        P(("group", "replica"), None),
        P(("group", "replica"), None),
        P(("group", "replica"), None),
        P(("group", "replica")),
        P(("group", "replica")),
        P(("group", "replica")),
    )
    return jax.shard_map(local, mesh=mesh, in_specs=in_specs, out_specs=out_specs, check_vma=False)
```

profile of v0, /device:TPU:0, one launch (start us, length us, event | category | flops | bytes accessed | tf_op | source)
XLA Modules:
  0.0 2042.5 jit_solution(7280609101151426072)
XLA Ops:
  7.2 2.1 convert_element_type.132
  11.0 43.8 %all-reduce = bf16[4352]{0:T(1024)(128)(2,1)S(1)} all-reduce(bf16[4352]{0:T(1024)(128)(2,1)S(1)} %dynamic-update-slice), channel_id=1, replica_groups=mesh['group'=4,'replica'=8] {'group','replica'}, use_global_device_ids=true, to_apply=%add | all-reduce | flops 4352 | bytes 17408
  54.7 1.2 fusion.48
  56.4 73.6 %all-gather.7.cloned.1.call-done = bf16[2048,4096]{1,0:T(8,128)(2,1)} async-done(((bf16[64,4096]{1,0:T(8,128)(2,1)}), bf16[2048,4096]{1,0:T(8,128)(2,1)}) %all-gather.7.cloned.1.call-update) | async-done | bytes 16777232 | tf_op jit(solution)/shard_map/all_gather | solution.py:118
  130.0 8.2 fusion.70
  138.2 1.3 copy-done.4
  141.5 1.1 slice.124
  144.3 3.2 convert_element_type.142
  147.6 2.4 convert_element_type.144
  150.9 1.3 slice_bitcast_fusion
  154.6 14.4 all-gather.9.cloned.1.call-done
  169.0 2.9 fusion.2
  171.9 3.2 copy-done
  175.1 1.7 fusion.4
  176.8 24.4 %all-gather.11.cloned.1.call-done = bf16[1024,8,128]{0,2,1:T(8,128)(2,1)} async-done(((bf16[128,8,128]{0,2,1:T(8,128)(2,1)}), bf16[1024,8,128]{0,2,1:T(8,128)(2,1)}) %all-gather.11.cloned.1.call-update) | async-done | bytes 2097168 | tf_op jit(solution)/shard_map/all_gather | solution.py:147
  201.2 5.8 divide_convert_fusion
  207.0 73.8 %all-gather.13.cloned.1.call-done = bf16[2048,2048]{1,0:T(8,128)(2,1)} async-done(((bf16[64,2048]{1,0:T(8,128)(2,1)}), bf16[2048,2048]{1,0:T(8,128)(2,1)}) %all-gather.13.cloned.1.call-update) | async-done | bytes 8388624 | tf_op jit(solution)/shard_map/all_gather | solution.py:119
  280.7 4.7 multiply_reduce_fusion.4
  285.5 272.1 %all-gather.15.cloned.1.call-done = bf16[2048,12288]{1,0:T(8,128)(2,1)} async-done(((bf16[64,12288]{1,0:T(8,128)(2,1)}), bf16[2048,12288]{1,0:T(8,128)(2,1)}) %all-gather.15.cloned.1.call-update) | async-done | bytes 50331664 | tf_op jit(solution)/shard_map/all_gather | solution.py:174
  557.6 21.5 %fusion.91 = f32[128,12288]{1,0:T(8,128)} fusion(bf16[2048,12288]{1,0:T(8,128)(2,1)} %all-gather.15.cloned.1.call-done, f32[128,2048]{1,0:T(8,128)S(1)} %get-tuple-element.86, f32[2048]{0:T(1024)S(1)} %get-tuple-element.75, f32[128]{0:T(128)S(1)} %add_rsqrt_fusion.2), kind=kOutput, calls=%fused_computation.194 | convolution fusion | flops 6443237376 | bytes 57680384 | tf_op jit(solution)/shard_map/dot_general | solution.py:179
  579.1 134.2 %all-gather.17.cloned.1.call-done = bf16[6144,2048]{1,0:T(8,128)(2,1)} async-done(((bf16[192,2048]{1,0:T(8,128)(2,1)}), bf16[6144,2048]{1,0:T(8,128)(2,1)}) %all-gather.17.cloned.1.call-update) | async-done | bytes 25165840 | tf_op jit(solution)/shard_map/all_gather | solution.py:177
  713.4 16.3 multiply_convert_fusion.2
  729.7 24.6 %multiply_reduce_fusion = (bf16[2048]{0:T(1024)(128)(2,1)}, f32[128]{0:T(128)S(1)}, f32[128,2048]{1,0:T(8,128)}) fusion(f32[128,2048]{1,0:T(8,128)S(1)} %get-tuple-element.86, f32[128]{0:T(128)S(1)} %add_rsqrt_fusion.2, f32[2048]{0:T(1024)S(1)} %get-tuple-element.75, bf16[2048,12288]{1,0:T(8,128)(2,1)} %all-gather.15.cloned.1.call-done, ...), kind=kOutput, calls=%fused_computation.82 | convolution fusion | flops 6450313216 | bytes 55587840 | tf_op jit(solution)/shard_map/dot_general | solution.py:192
  754.2 1.7 multiply_add_fusion.4
  755.9 7.1 convolution_convert_fusion.4
  763.0 2.0 copy.144
  765.0 1.4 multiply_reduce_fusion.2
  766.4 6.6 bitcast_convert_fusion
  773.0 5.1 multiply_convert_fusion
  778.2 2.8 bitcast_convert_fusion.1
  781.0 3.9 copy.180
  785.0 3.9 copy.181
  788.9 4.6 pad_maximum_fusion
  793.6 6.6 convolution_convert_fusion.3
  802.1 3.8 fusion.34
  805.9 1.0 fusion.98
  806.9 2.4 copy.182
  809.3 2.4 copy.183
  811.8 1.8 multiply_add_fusion.3
  813.6 1.0 multiply_reduce_fusion.1
  815.3 2.7 fusion.53
  818.1 23.7 %reduce-scatter.10.cloned.1.call-done = bf16[128,2,1024]{2,0,1:T(8,128)(2,1)} async-done(((bf16[1024,2,1024]{2,0,1:T(8,128)(2,1)}), bf16[128,2,1024]{2,0,1:T(8,128)(2,1)}) %reduce-scatter.10.cloned.1.call-update) | async-done | bytes 524304 | tf_op jit(solution)/shard_map/reduce_scatter | solution.py:244
  841.7 1.8 convert_bitcast_fusion
  844.1 1.1 fusion.68
  845.7 2.2 fusion.63
  848.0 9.6 convolution_convert_fusion.2
  858.6 13.8 convolution_convert_fusion.1
  873.1 22.4 %convolution_convert_fusion = bf16[2048,12288]{1,0:T(8,128)(2,1)} fusion(bf16[128,6144]{1,0:T(8,128)(2,1)} %get-tuple-element.51, bf16[128,6144]{1,0:T(8,128)(2,1)} %get-tuple-element.50, f32[128,2048]{1,0:T(8,128)S(1)} %get-tuple-element.86, f32[2048]{0:T(1024)S(1)} %get-tuple-element.75, f32[128]{0:T(128)S(1)} %copy-done.22), kind=kOutput, calls=%fused_computation | convolution fusion | flops 6474694656 | bytes 54534656 | tf_op jit(solution)/shard_map/dot_general | solution.py:194
  895.5 34.1 %reduce-scatter.16.cloned.1.call-done = bf16[512,2048]{1,0:T(8,128)(2,1)} async-done(((bf16[2048,2048]{1,0:T(8,128)(2,1)}), bf16[512,2048]{1,0:T(8,128)(2,1)}) %reduce-scatter.16.cloned.1.call-update) | async-done | bytes 2097168 | tf_op jit(solution)/shard_map/reduce_scatter | solution.py:275
  929.7 156.8 %reduce-scatter.12.cloned.1.call-done = bf16[512,4096]{1,0:T(8,128)(2,1)} async-done(((bf16[2048,4096]{1,0:T(8,128)(2,1)}), bf16[512,4096]{1,0:T(8,128)(2,1)}) %reduce-scatter.12.cloned.1.call-update) | async-done | bytes 4194320 | tf_op jit(solution)/shard_map/reduce_scatter | solution.py:272
  1086.5 224.6 %reduce-scatter.24.cloned.1.call-done = bf16[1536,2048]{1,0:T(8,128)(2,1)} async-done(((bf16[6144,2048]{1,0:T(8,128)(2,1)}), bf16[1536,2048]{1,0:T(8,128)(2,1)}) %reduce-scatter.24.cloned.1.call-update) | async-done | bytes 6291472 | tf_op jit(solution)/shard_map/reduce_scatter | solution.py:203
  1311.5 426.8 %reduce-scatter.20.cloned.1.call-done = bf16[512,12288]{1,0:T(8,128)(2,1)} async-done(((bf16[2048,12288]{1,0:T(8,128)(2,1)}), bf16[512,12288]{1,0:T(8,128)(2,1)}) %reduce-scatter.20.cloned.1.call-update) | async-done | bytes 12582928 | tf_op jit(solution)/shard_map/reduce_scatter | solution.py:200
  1741.5 13.1 fusion.19
  1754.7 12.6 fusion.47
  1767.4 15.2 all-reduce.1
  1782.7 14.7 all-reduce.2
  1798.1 2.7 fusion.46
  1800.8 2.7 multiply_subtract_fusion.5
  1803.5 24.2 %reduce-scatter.14.cloned.1.call-done = bf16[64,4096]{1,0:T(8,128)(2,1)} async-done(((bf16[512,4096]{1,0:T(8,128)(2,1)}), bf16[64,4096]{1,0:T(8,128)(2,1)}) %reduce-scatter.14.cloned.1.call-update) | async-done | bytes 524304 | tf_op jit(solution)/shard_map/reduce_scatter | solution.py:283
  1827.7 4.0 multiply_subtract_fusion.2
  1831.6 66.4 %reduce-scatter.26.cloned.1.call-done = bf16[192,2048]{1,0:T(8,128)(2,1)} async-done(((bf16[1536,2048]{1,0:T(8,128)(2,1)}), bf16[192,2048]{1,0:T(8,128)(2,1)}) %reduce-scatter.26.cloned.1.call-update) | async-done | bytes 786448 | tf_op jit(solution)/shard_map/reduce_scatter | solution.py:295
  1898.0 5.3 multiply_subtract_fusion.1
  1903.3 124.5 %reduce-scatter.22.cloned.1.call-done = bf16[64,12288]{1,0:T(8,128)(2,1)} async-done(((bf16[512,12288]{1,0:T(8,128)(2,1)}), bf16[64,12288]{1,0:T(8,128)(2,1)}) %reduce-scatter.22.cloned.1.call-update) | async-done | bytes 1572880 | tf_op jit(solution)/shard_map/reduce_scatter | solution.py:292
  2027.8 7.7 multiply_subtract_fusion
  (172 shorter events, 16.7 us)
Async XLA Ops:
  7.2 122.8 %copy-start.2 = (bf16[128,2048]{1,0:T(8,128)(2,1)S(1)}, bf16[128,2048]{1,0:T(8,128)(2,1)}, u32[]{:S(2)}) copy-start(bf16[128,2048]{1,0:T(8,128)(2,1)} %param.20) | copy-start | bytes 1572868
  7.2 122.8 %all-gather.7.cloned.1.call-start = ((), (), s32[]{:S(2)}) async-start(), calls=%async_computation.9 | async-start | bytes 17301504 | tf_op jit(solution)/shard_map/all_gather | solution.py:118
  9.4 159.6 %all-gather.9.cloned.1.call-start = ((), (), s32[]{:S(2)}) async-start(), calls=%async_computation.10 | async-start | bytes 2359296 | tf_op jit(solution)/shard_map/all_gather | solution.py:146
  56.0 82.2 %copy-start.29 = (f32[128]{0:T(128)}, f32[128]{0:T(128)S(1)}, u32[]{:S(2)}) copy-start(f32[128]{0:T(128)S(1)} %add_rsqrt_fusion.3) | copy-start | bytes 1540
  56.0 84.1 %copy-start.31 = (f32[128]{0:T(128)}, f32[128]{0:T(128)S(1)}, u32[]{:S(2)}) copy-start(f32[128]{0:T(128)S(1)} %get-tuple-element.77) | copy-start | bytes 1540
  56.0 96.8 %copy-start.34 = (f32[128]{0:T(128)}, f32[128]{0:T(128)S(1)}, u32[]{:S(2)}) copy-start(f32[128]{0:T(128)S(1)} %get-tuple-element.78) | copy-start | bytes 1540
  138.2 1.3 copy-start.4
  139.7 3.8 copy-start.11
  139.8 3.7 copy-start.17
  140.1 7.4 copy-start.23
  141.4 59.7 %all-gather.11.cloned.1.call-start = ((), (), s32[]{:S(2)}) async-start(), calls=%async_computation.11 | async-start | bytes 2359296 | tf_op jit(solution)/shard_map/all_gather | solution.py:147
  143.4 137.3 %all-gather.13.cloned.1.call-start = ((), (), s32[]{:S(2)}) async-start(), calls=%async_computation.12 | async-start | bytes 8650752 | tf_op jit(solution)/shard_map/all_gather | solution.py:119
  144.3 413.4 %all-gather.15.cloned.1.call-start = ((), (), s32[]{:S(2)}) async-start(), calls=%async_computation.13 | async-start | bytes 51904512 | tf_op jit(solution)/shard_map/all_gather | solution.py:174
  147.5 2.8 copy-start.39
  147.5 565.8 %all-gather.17.cloned.1.call-start = ((), (), s32[]{:S(2)}) async-start(), calls=%async_computation.14 | async-start | bytes 25952256 | tf_op jit(solution)/shard_map/all_gather | solution.py:177
  150.0 691.7 %reduce-scatter.10.cloned.1.call-start = ((), (), s32[]{:S(2)}) async-start(), calls=%async_computation.15 | async-start | bytes 4718592 | tf_op jit(solution)/shard_map/reduce_scatter | solution.py:244
  154.6 17.3 copy-start.8
  171.8 3.2 copy-start
  206.9 78.5 %copy-start.6 = (bf16[128,8,2,128]{0,3,2,1:T(8,128)(2,1)}, bf16[128,8,2,128]{0,3,2,1:T(8,128)(2,1)S(1)}, u32[]{:S(2)}) copy-start(bf16[128,8,2,128]{0,3,2,1:T(8,128)(2,1)S(1)} %divide_convert_fusion) | copy-start | bytes 1572868
  285.5 468.8 %copy-start.21 = (f32[128]{0:T(128)}, f32[128]{0:T(128)S(1)}, u32[]{:S(2)}) copy-start(f32[128]{0:T(128)S(1)} %add_rsqrt_fusion.2) | copy-start | bytes 1540
  557.6 155.7 %copy-start.14 = (bf16[128,2048]{1,0:T(8,128)(2,1)S(1)}, bf16[128,2048]{1,0:T(8,128)(2,1)}, u32[]{:S(2)}) copy-start(bf16[128,2048]{1,0:T(8,128)(2,1)} %param.21) | copy-start | bytes 1572868
  766.4 6.6 copy-start.7
  766.4 6.6 copy-start.19
  773.0 5.2 copy-start.9
  778.2 2.8 copy-start.1
  793.5 136.1 %reduce-scatter.16.cloned.1.call-start = ((), (), s32[]{:S(2)}) async-start(), calls=%async_computation.18 | async-start | bytes 10485760 | tf_op jit(solution)/shard_map/reduce_scatter | solution.py:275
  800.1 0.7 copy-start.32
  800.1 1.2 copy-start.35
  800.1 1.9 copy-start.24
  800.1 286.3 %reduce-scatter.12.cloned.1.call-start = ((), (), s32[]{:S(2)}) async-start(), calls=%async_computation.16 | async-start | bytes 20971520 | tf_op jit(solution)/shard_map/reduce_scatter | solution.py:272
  813.6 1.7 copy-start.5
  813.6 1.7 copy-start.27
  818.0 26.0 %copy-start.12 = (f32[16,8,8,128]{3,2,1,0:T(8,128)S(1)}, f32[16,8,8,128]{3,2,1,0:T(8,128)}, u32[]{:S(2)}) copy-start(f32[16,8,8,128]{3,2,1,0:T(8,128)} %copy-done.11) | copy-start | bytes 1572868
  818.0 26.0 %copy-start.25 = (f32[128,8]{0,1:T(8,128)S(1)}, f32[128,8]{0,1:T(8,128)}, u32[]{:S(2)}) copy-start(f32[128,8]{0,1:T(8,128)} %copy-done.23) | copy-start | bytes 12292
  818.0 26.0 %copy-start.33 = (f32[128]{0:T(128)S(1)}, f32[128]{0:T(128)}, u32[]{:S(2)}) copy-start(f32[128]{0:T(128)} %copy-done.31) | copy-start | bytes 1540
  844.0 3.9 copy-start.3
  844.1 3.9 copy-start.20
  857.5 1.0 copy-start.15
  857.6 453.6 %reduce-scatter.24.cloned.1.call-start = ((), (), s32[]{:S(2)}) async-start(), calls=%async_computation.22 | async-start | bytes 31457280 | tf_op jit(solution)/shard_map/reduce_scatter | solution.py:203
  872.4 0.7 copy-start.22
  872.4 865.8 %reduce-scatter.20.cloned.1.call-start = ((), (), s32[]{:S(2)}) async-start(), calls=%async_computation.20 | async-start | bytes 62914560 | tf_op jit(solution)/shard_map/reduce_scatter | solution.py:200
  895.5 905.3 %reduce-scatter.18.cloned.1.call-start = ((), (), s32[]{:S(2)}) async-start(), calls=%async_computation.19 | async-start | bytes 2359296 | tf_op jit(solution)/shard_map/reduce_scatter | solution.py:286
  929.6 898.0 %reduce-scatter.14.cloned.1.call-start = ((), (), s32[]{:S(2)}) async-start(), calls=%async_computation.17 | async-start | bytes 4718592 | tf_op jit(solution)/shard_map/reduce_scatter | solution.py:283
  1086.5 811.5 %reduce-scatter.26.cloned.1.call-start = ((), (), s32[]{:S(2)}) async-start(), calls=%async_computation.23 | async-start | bytes 7077888 | tf_op jit(solution)/shard_map/reduce_scatter | solution.py:295
  1311.2 716.6 %reduce-scatter.22.cloned.1.call-start = ((), (), s32[]{:S(2)}) async-start(), calls=%async_computation.21 | async-start | bytes 14155776 | tf_op jit(solution)/shard_map/reduce_scatter | solution.py:292
  1738.2 0.8 copy-start.41
  1738.2 1.4 copy-start.40
  1738.2 3.3 copy-start.26
  1741.5 13.2 copy-start.16
  1741.5 13.2 copy-start.30
  1754.7 12.7 copy-start.28
  1754.7 42.7 %copy-start.36 = (f32[136]{0:T(256)S(1)}, f32[136]{0:T(256)}, u32[]{:S(2)}) copy-start(f32[136]{0:T(256)} %param.37) | copy-start | bytes 1636
  1754.7 42.7 %copy-start.37 = (f32[136]{0:T(256)S(1)}, f32[136]{0:T(256)}, u32[]{:S(2)}) copy-start(f32[136]{0:T(256)} %param.39) | copy-start | bytes 1636
  1754.7 42.7 %copy-start.38 = (f32[136]{0:T(256)S(1)}, f32[136]{0:T(256)}, u32[]{:S(2)}) copy-start(f32[136]{0:T(256)} %param.38) | copy-start | bytes 1636
  1767.4 33.4 %copy-start.18 = (f32[64,2048]{1,0:T(8,128)S(1)}, f32[64,2048]{1,0:T(8,128)}, u32[]{:S(2)}) copy-start(f32[64,2048]{1,0:T(8,128)} %param.28) | copy-start | bytes 1572868
  1798.1 29.6 %copy-start.13 = (f32[64,4096]{1,0:T(8,128)S(1)}, f32[64,4096]{1,0:T(8,128)}, u32[]{:S(2)}) copy-start(f32[64,4096]{1,0:T(8,128)} %param.25) | copy-start | bytes 3145732
  1803.5 94.5 %copy-start.10 = (f32[192,2048]{1,0:T(8,128)S(1)}, f32[192,2048]{1,0:T(8,128)}, u32[]{:S(2)}) copy-start(f32[192,2048]{1,0:T(8,128)} %param.34) | copy-start | bytes 4718596
Sparse Core Ops, SparseCore 0:
  11.6 118.3 all-gather.6
  141.6 27.3 all-gather.8
  171.1 29.9 all-gather.10
  204.6 76.0 all-gather.12
  284.1 273.4 all-gather.14
  561.1 152.2 all-gather.16
  793.6 48.0 reduce-scatter.9
  844.8 84.7 reduce-scatter.15
  932.7 153.7 reduce-scatter.11
  1089.4 221.6 reduce-scatter.23
  1314.2 423.9 reduce-scatter.19
  1740.4 36.0 reduce-scatter.17
  1778.8 48.8 reduce-scatter.13
  1829.8 68.1 reduce-scatter.25
  1900.1 127.5 reduce-scatter.21
where the time goes:
time: 2050 us; the launch traced here: 2040 us
  waiting for transfers between devices  1670 us (81%)
  matrix products  187 us (9%)
  blocking collectives  73.6 us (4%)
  other arithmetic  58.2 us (3%)
  local copies, waits for them, and re-layouts  31 us (2%)
    reduce_scatter x1, waiting for transfers between devices, local(): lax.psum_scatter(grad_gate_up_part.astype(jnp.bfloat16), 'group', scatter...  427 us
    all_gather x1, waiting for transfers between devices, local(): lax.all_gather(weight_gate_up.astype(jnp.bfloat16), ('group', 'replica'),...  272 us
    reduce_scatter x1, waiting for transfers between devices, local(): lax.psum_scatter(grad_down_part.astype(jnp.bfloat16), 'group', scatter_di...  225 us
    reduce_scatter x1, waiting for transfers between devices, local(): lax.psum_scatter(grad_qkv_part.astype(jnp.bfloat16), 'group', scatter_dim...  157 us
    all_gather x1, waiting for transfers between devices, local(): lax.all_gather(weight_down.astype(jnp.bfloat16), ('group', 'replica'), ax...  134 us
    reduce_scatter x1, waiting for transfers between devices, local(): lax.psum_scatter(mlp_shares[0].astype(jnp.bfloat16), 'replica', scatter_d...  124 us
    all_gather x1, waiting for transfers between devices, local(): lax.all_gather(weight_out.astype(jnp.bfloat16), ('group', 'replica'), axi...  73.8 us
    unnamed x3, blocking collectives  73.6 us
  transfers between devices with their start and end apart: 15, of which 14 were waited for; matrix products, arithmetic and copies ran while one was open for 8% of the time, Pallas kernels for 0%

commit v1 on v0

v1 whole, which is shorter than its diff:
```python
import jax
import jax.numpy as jnp
from jax import lax
from jax.sharding import PartitionSpec as P

HD = 128
KV_RATIO = 2
C = 128
SPG = 1

norm_eps = 1e-06
rope_base = 1000000.0
learn_rate = 0.1
beta_first = 0.9
beta_second = 0.95
adam_eps = 1e-08
decay_rate = 0.1
masked_score = -1e30
BF = jnp.bfloat16
F32 = jnp.float32


def rms_scale(values):
    return lax.rsqrt(jnp.mean(values * values, axis=-1, keepdims=True) + norm_eps)


def norm_back(grad_normed, normed, scale):
    return scale * (grad_normed - normed * jnp.mean(grad_normed * normed, axis=-1, keepdims=True))


def rope_tables(token_pos):
    half_dim = HD // 2
    frequency = rope_base ** (-(jnp.arange(half_dim).astype(F32) * 2.0 / HD))
    angles = token_pos.astype(F32)[:, None] * frequency[None, :]
    return (jnp.cos(angles)[:, None, :], jnp.sin(angles)[:, None, :])


def rotate(vectors, cosine, sine_table):
    half_dim = vectors.shape[-1] // 2
    first_half = vectors[..., :half_dim]
    second_half = vectors[..., half_dim:]
    return jnp.concatenate(
        [
            first_half * cosine - second_half * sine_table,
            second_half * cosine + first_half * sine_table,
        ],
        axis=-1,
    )


def unrotate(gradients, cosine, sine_table):
    return rotate(gradients, cosine, -sine_table)


def adam_step(weight, first_moment, second, gradient, step_value, decay_value):
    new_first = beta_first * first_moment + (1.0 - beta_first) * gradient
    new_second = beta_second * second + (1.0 - beta_second) * gradient * gradient
    first_hat = new_first / (1.0 - beta_first**step_value)
    second_hat = new_second / (1.0 - beta_second**step_value)
    new_weight = weight - learn_rate * (
        first_hat / (jnp.sqrt(second_hat) + adam_eps) + decay_value * weight
    )
    return (new_weight, new_first, new_second)


def dot(a, b):
    return jnp.dot(a, b, preferred_element_type=F32)


def dot_nt(a, b):
    return lax.dot_general(a, b, (((1,), (1,)), ((), ())), preferred_element_type=F32)


def dot_tn(a, b):
    return lax.dot_general(a, b, (((0,), (0,)), ((), ())), preferred_element_type=F32)


def gather_rows(block):
    return lax.all_gather(block, "replica", axis=0, tiled=True)


def scatter_rows(partial):
    return lax.psum_scatter(
        partial.astype(BF), "replica", scatter_dimension=0, tiled=True
    ).astype(F32)


def swap_blocks(blocks):
    return lax.all_to_all(blocks, "replica", 0, 0, tiled=True)


def make_local(groups, replicas):
    sub_count = replicas // groups
    sub_groups = [[s * groups + k for k in range(groups)] for s in range(sub_count)]
    slice_of = [(r % groups) * sub_count + r // groups for r in range(replicas)]

    def swap_sub(blocks):
        return lax.all_to_all(
            blocks, "replica", 0, 0, axis_index_groups=sub_groups, tiled=True
        )

    def gather_group(block):
        return lax.all_gather(block, "group", axis=0, tiled=True)

    def scatter_group(partial):
        return lax.psum_scatter(partial.astype(BF), "group", scatter_dimension=0, tiled=True)

    def local(
        inputs,
        cotangent,
        block_map,
        positions,
        step_count,
        weight_qkv,
        first_qkv,
        second_qkv,
        weight_out,
        first_out,
        second_out,
        weight_gate_up,
        first_gate_up,
        second_gate_up,
        weight_down,
        first_down,
        second_down,
        norm_gains,
        first_gains,
        second_gains,
    ):
        tok_rows, width = inputs.shape
        seq_rows = tok_rows * replicas
        own_rows = weight_qkv.shape[0]
        own_ff = weight_down.shape[0]
        heads = weight_out.shape[0] * groups * replicas // HD
        kv_heads = heads // KV_RATIO
        q_cols = heads * HD
        kv_cols = kv_heads * HD
        q_per = heads // replicas
        kv_per = max(1, kv_heads // replicas)
        ratio = q_per // kv_per
        kv_start = [slice_of[r] * q_per // KV_RATIO for r in range(replicas)]
        attn_scale = HD ** (-0.5)
        map_row = block_map[0]
        seq_len = map_row.shape[0] * C // SPG

        down_slice = gather_group(weight_down.astype(BF))
        qkv_b = weight_qkv.astype(BF)
        qkv_blocks = jnp.stack(
            [
                jnp.concatenate(
                    [
                        qkv_b[:, slice_of[r] * q_per * HD : (slice_of[r] + 1) * q_per * HD],
                        qkv_b[:, q_cols + kv_start[r] * HD : q_cols + (kv_start[r] + kv_per) * HD],
                        qkv_b[
                            :,
                            q_cols + kv_cols + kv_start[r] * HD : q_cols
                            + kv_cols
                            + (kv_start[r] + kv_per) * HD,
                        ],
                    ],
                    axis=1,
                )
                for r in range(replicas)
            ]
        )
        qkv_slice = gather_group(
            swap_blocks(qkv_blocks).reshape(replicas * own_rows, qkv_blocks.shape[2])
        )
        gu_blocks = (
            weight_gate_up.astype(BF)
            .reshape(own_rows, 2, groups, replicas, own_ff)
            .transpose(3, 0, 1, 2, 4)
            .reshape(replicas, own_rows, 2 * groups * own_ff)
        )
        gu_slice = gather_group(
            swap_blocks(gu_blocks).reshape(replicas * own_rows, gu_blocks.shape[2])
        )
        out_own = weight_out.shape[0]
        out_all = gather_group(weight_out.astype(BF)[None])
        out_slice = swap_sub(out_all).reshape(groups * out_own, width)
        ff_slice = groups * own_ff

        gains_full = lax.all_gather(
            norm_gains.astype(BF), ("group", "replica"), axis=0, tiled=True
        ).astype(F32)
        gain_one = gains_full[:width]
        gain_two = gains_full[width : 2 * width]
        gain_query = gains_full[2 * width : 2 * width + HD]
        gain_key = gains_full[2 * width + HD :]

        pos_all = lax.all_gather(positions, "replica", axis=0, tiled=True)
        row_ids = jnp.arange(seq_rows, dtype=jnp.int32)
        slot_hot = (row_ids // C)[:, None] == jnp.arange(map_row.shape[0], dtype=jnp.int32)[None, :]
        ordinals = (
            jnp.sum(jnp.where(slot_hot, map_row[None, :], 0), axis=1) * C + row_ids % C
        )
        allowed = (ordinals[None, :] // seq_len == ordinals[:, None] // seq_len) & (
            ordinals[None, :] <= ordinals[:, None]
        )
        cosine, sine_table = rope_tables(pos_all)

        x_all = gather_rows(inputs).astype(F32)
        cot_all = gather_rows(cotangent)
        hidden_one = (x_all * rms_scale(x_all) * gain_one).astype(BF)
        projected = dot(hidden_one, qkv_slice)
        query_raw = projected[:, : q_per * HD].reshape(seq_rows, q_per, HD)
        key_raw = projected[:, q_per * HD : (q_per + kv_per) * HD].reshape(seq_rows, kv_per, HD)
        value_rows = (
            projected[:, (q_per + kv_per) * HD :].reshape(seq_rows, kv_per, HD).astype(BF)
        )
        query_scale = rms_scale(query_raw)
        query_hat = query_raw * query_scale
        key_scale = rms_scale(key_raw)
        key_hat = key_raw * key_scale
        query_rot = (rotate(query_hat * gain_query, cosine, sine_table) * attn_scale).astype(BF)
        key_rot = rotate(key_hat * gain_key, cosine, sine_table).astype(BF)
        query_groups = query_rot.reshape(seq_rows, kv_per, ratio, HD)
        scores = jnp.einsum(
            "qgrd,kgd->grqk", query_groups, key_rot, preferred_element_type=F32
        )
        scores = jnp.where(allowed, scores, masked_score)
        row_max = jnp.max(scores, axis=-1)
        attn_probs = jnp.where(allowed, jnp.exp(scores - row_max[..., None]), 0.0)
        row_sum = jnp.sum(attn_probs, axis=-1)
        mixed_part = jnp.einsum(
            "grqk,kgd->grqd", attn_probs.astype(BF), value_rows, preferred_element_type=F32
        )
        log_total = row_max + jnp.log(row_sum)
        mixed = (
            (mixed_part / row_sum[..., None])
            .transpose(2, 0, 1, 3)
            .reshape(seq_rows, q_per * HD)
            .astype(BF)
        )
        x_own = inputs.astype(F32)
        resid_one = x_own + scatter_rows(dot(mixed, out_slice))
        scale_two = rms_scale(resid_one)
        normed_two = resid_one * scale_two
        hidden_two = gather_rows((normed_two * gain_two).astype(BF))

        gate_up = dot(hidden_two, gu_slice)
        gate_in = gate_up[:, :ff_slice]
        up_in = gate_up[:, ff_slice:]
        sigmoid_gate = jax.nn.sigmoid(gate_in)
        silu_gate = gate_in * sigmoid_gate
        activated = (silu_gate * up_in).astype(BF)
        block_part = dot(activated, down_slice)
        act_grad = dot_nt(cot_all, down_slice)
        gate_grad = act_grad * up_in * sigmoid_gate * (1.0 + gate_in * (1.0 - sigmoid_gate))
        up_grad = act_grad * silu_gate
        gate_up_grad = jnp.concatenate([gate_grad, up_grad], axis=1).astype(BF)
        hidden_two_grad = scatter_rows(dot_nt(gate_up_grad, gu_slice))
        block_out = (resid_one + scatter_rows(block_part)).astype(BF)
        gain_two_grad = jnp.sum(hidden_two_grad * normed_two, axis=0)
        resid_grad = cotangent.astype(F32) + norm_back(
            hidden_two_grad * gain_two, normed_two, scale_two
        )
        attn_grad = gather_rows(resid_grad.astype(BF))

        grad_down = scatter_group(dot_tn(activated, cot_all)).astype(F32)
        gu_mid = scatter_group(dot_tn(hidden_two, gate_up_grad))
        grad_gate_up = (
            swap_blocks(gu_mid.reshape(replicas, own_rows, 2 * ff_slice))
            .reshape(replicas, own_rows, 2, groups, own_ff)
            .transpose(1, 2, 3, 0, 4)
            .reshape(own_rows, 2 * groups * replicas * own_ff)
            .astype(F32)
        )

        mixed_grad = dot_nt(attn_grad, out_slice).astype(BF)
        grad_out_part = dot_tn(mixed, attn_grad).astype(BF).reshape(groups, out_own, width)
        grad_out = scatter_group(swap_sub(grad_out_part))[0].astype(F32)
        mixed_grad_groups = mixed_grad.reshape(seq_rows, kv_per, ratio, HD).transpose(1, 2, 0, 3)
        row_delta = jnp.sum(
            (mixed_grad.astype(F32) * mixed.astype(F32)).reshape(seq_rows, kv_per, ratio, HD),
            axis=-1,
        ).transpose(1, 2, 0)
        probs = jnp.where(allowed, jnp.exp(scores - log_total[..., None]), 0.0)
        value_grad = jnp.einsum(
            "grqk,grqd->kgd", probs.astype(BF), mixed_grad_groups, preferred_element_type=F32
        )
        prob_grad = jnp.einsum(
            "grqd,kgd->grqk", mixed_grad_groups, value_rows, preferred_element_type=F32
        )
        score_grad = (probs * (prob_grad - row_delta[..., None])).astype(BF)
        query_grad = jnp.einsum(
            "grqk,kgd->qgrd", score_grad, key_rot, preferred_element_type=F32
        ).reshape(seq_rows, q_per, HD)
        key_grad = jnp.einsum(
            "grqk,qgrd->kgd", score_grad, query_groups, preferred_element_type=F32
        )
        query_norm_grad = unrotate(query_grad * attn_scale, cosine, sine_table)
        gain_query_grad = jnp.sum(query_norm_grad * query_hat, axis=(0, 1))
        query_raw_grad = norm_back(query_norm_grad * gain_query, query_hat, query_scale)
        key_norm_grad = unrotate(key_grad, cosine, sine_table)
        gain_key_grad = jnp.sum(key_norm_grad * key_hat, axis=(0, 1))
        key_raw_grad = norm_back(key_norm_grad * gain_key, key_hat, key_scale)
        projected_grad = jnp.concatenate(
            [
                query_raw_grad.reshape(seq_rows, q_per * HD),
                key_raw_grad.reshape(seq_rows, kv_per * HD),
                value_grad.reshape(seq_rows, kv_per * HD),
            ],
            axis=1,
        ).astype(BF)
        qkv_mid = scatter_group(dot_tn(hidden_one, projected_grad))
        qkv_back = swap_blocks(qkv_mid.reshape(replicas, own_rows, qkv_mid.shape[1])).astype(F32)
        q_at = [slice_of.index(j) for j in range(replicas)]
        shares = [
            [r for r in range(replicas) if kv_start[r] <= m < kv_start[r] + kv_per]
            for m in range(kv_heads)
        ]

        def kv_part(offset):
            pieces = []
            for m in range(kv_heads):
                terms = [
                    qkv_back[r][
                        :,
                        offset + (m - kv_start[r]) * HD : offset + (m - kv_start[r] + 1) * HD,
                    ]
                    for r in shares[m]
                ]
                pieces.append(sum(terms[1:], terms[0]))
            return pieces

        grad_qkv = jnp.concatenate(
            [qkv_back[r][:, : q_per * HD] for r in q_at]
            + kv_part(q_per * HD)
            + kv_part((q_per + kv_per) * HD),
            axis=1,
        )
        hidden_one_grad = scatter_rows(dot_nt(projected_grad, qkv_slice))
        scale_one = rms_scale(x_own)
        normed_one = x_own * scale_one
        gain_one_grad = jnp.sum(hidden_one_grad * normed_one, axis=0)
        input_grad = resid_grad + norm_back(hidden_one_grad * gain_one, normed_one, scale_one)
        grad_gains_part = jnp.concatenate(
            [gain_one_grad, gain_two_grad, gain_query_grad, gain_key_grad]
        )
        grad_gains = lax.psum_scatter(
            grad_gains_part, ("group", "replica"), scatter_dimension=0, tiled=True
        )

        step_value = step_count[0].astype(F32)
        new_qkv = adam_step(weight_qkv, first_qkv, second_qkv, grad_qkv, step_value, decay_rate)
        new_out = adam_step(weight_out, first_out, second_out, grad_out, step_value, decay_rate)
        new_gu = adam_step(
            weight_gate_up, first_gate_up, second_gate_up, grad_gate_up, step_value, decay_rate
        )
        new_down = adam_step(
            weight_down, first_down, second_down, grad_down, step_value, decay_rate
        )
        new_gains = adam_step(norm_gains, first_gains, second_gains, grad_gains, step_value, 0.0)
        return (
            block_out,
            input_grad,
            grad_qkv,
            grad_out,
            grad_gate_up,
            grad_down,
            grad_gains,
            *new_qkv,
            *new_out,
            *new_gu,
            *new_down,
            *new_gains,
        )

    return local


def solution(mesh):
    both = ("group", "replica")
    rows = P(both, None)
    flat = P(both)
    in_specs = (rows, rows, P("group", None), flat, P()) + (rows,) * 12 + (flat,) * 3
    out_specs = (rows,) * 6 + (flat,) + (rows,) * 12 + (flat,) * 3
    local = make_local(mesh.shape["group"], mesh.shape["replica"])
    return jax.shard_map(local, mesh=mesh, in_specs=in_specs, out_specs=out_specs, check_vma=False)
```

time: 2050 us -> 877 us (0.43)
  waiting for transfers between devices: 1670 us -> 435 us
  blocking collectives: 73.6 us -> 193 us
  matrix products: 187 us -> 110 us
    reduce_scatter x9 -> x7, waiting for transfers between devices: 1080 us -> 164 us  [the longest x4 104 us: scatter_rows(): lax.psum_scatter(partial.astype(BF), 'replica', scatter_dimension=0, tile...]
    all_gather x6 -> x8, waiting for transfers between devices: 593 us -> 252 us  [the longest x4 129 us: gather_group(): return lax.all_gather(block, 'group', axis=0, tiled=True)]
    all_to_all x0 -> x3, blocking collectives: none -> 102 us  [the longest x2 84.5 us: swap_blocks(): return lax.all_to_all(blocks, 'replica', 0, 0, tiled=True)]
    dot_general x17, matrix products: 185 us -> 106 us  [the longest x4 31.5 us: dot_nt(): lax.dot_general(a, b, (((1,), (1,)), ((), ())), preferred_element_type=F32)]
    unnamed x3 -> x2, blocking collectives: 73.6 us -> 81.3 us
  transfers between devices with their start and end apart: 15 -> 19, of which waited for: 14 -> 13; matrix products, arithmetic and copies ran while one was open for 8% -> 20% of each run, Pallas kernels for 0% -> 0%
where the time goes in v1:
time: 877 us; the launch traced here: 873 us
  waiting for transfers between devices  435 us (50%)
  blocking collectives  193 us (22%)
  matrix products  110 us (13%)
  other arithmetic  59.9 us (7%)
  local copies, waits for them, and re-layouts  43.1 us (5%)
  between operations  15.9 us (2%)
  starting transfers between devices  15 us (2%)
    all_gather x4, waiting for transfers between devices, gather_group(): return lax.all_gather(block, 'group', axis=0, tiled=True)  129 us
    all_gather x4, waiting for transfers between devices, gather_rows(): return lax.all_gather(block, 'replica', axis=0, tiled=True)  123 us
    reduce_scatter x4, waiting for transfers between devices, scatter_rows(): lax.psum_scatter(partial.astype(BF), 'replica', scatter_dimension=0, tile...  104 us
    all_to_all x2, blocking collectives, swap_blocks(): return lax.all_to_all(blocks, 'replica', 0, 0, tiled=True)  84.5 us
    unnamed x2, blocking collectives  81.3 us
    reduce_scatter x3, waiting for transfers between devices, scatter_group(): lax.psum_scatter(partial.astype(BF), 'group', scatter_dimension=0, tiled=...  60.3 us
    dot_general x4, matrix products, dot_nt(): lax.dot_general(a, b, (((1,), (1,)), ((), ())), preferred_element_type=F32)  31.5 us
    dot_general x4, matrix products, dot(): return jnp.dot(a, b, preferred_element_type=F32)  28.9 us
  transfers between devices with their start and end apart: 19, of which 13 were waited for; matrix products, arithmetic and copies ran while one was open for 20% of the time, Pallas kernels for 0%

profile of v1, /device:TPU:0, one launch (start us, length us, event | category | flops | bytes accessed | tf_op | source)
XLA Modules:
  0.0 872.5 jit_solution(8811267959033577495)
XLA Ops:
  7.2 1.8 convert_element_type.180
  11.4 21.6 %all_to_all.30 = bf16[8,64,512]{2,1,0:T(8,128)(2,1)} all-to-all(bf16[8,64,512]{2,1,0:T(8,128)(2,1)S(1)} %constant_dynamic-update-slice_fusion), channel_id=1, replica_groups=mesh['group'=4,'replica'=8] {'replica'}, dimensions={0} | all-to-all | bytes 1048576 | tf_op jit(solution)/shard_map/all_to_all | solution.py:89
  33.0 9.7 %all-gather.1 = s32[8,1,128]{2,1,0:T(1,128)S(1)} all-gather(s32[1,1,128]{2,1,0:T(1,128)S(1)} %bitcast.258), channel_id=1, replica_groups=mesh['group'=4,'replica'=8] {'replica'}, dimensions={0}, use_global_device_ids=true | all-gather | bytes 4608 | tf_op jit(solution)/shard_map/all_gather | solution.py:191
  42.9 41.8 %all-reduce = bf16[4352]{0:T(1024)(128)(2,1)S(1)} all-reduce(bf16[4352]{0:T(1024)(128)(2,1)S(1)} %dynamic-update-slice), channel_id=1, replica_groups=mesh['group'=4,'replica'=8] {'group','replica'}, use_global_device_ids=true, to_apply=%add | all-reduce | flops 4352 | bytes 17408
  84.8 3.2 fusion.76
  89.2 4.2 all-to-all-start.1
  93.7 3.1 fusion
  96.8 28.3 %all-gather.13.cloned.1.call-done = bf16[2048,512]{1,0:T(8,128)(2,1)} async-done(((bf16[512,512]{1,0:T(8,128)(2,1)}), bf16[2048,512]{1,0:T(8,128)(2,1)}) %all-gather.13.cloned.1.call-update) | async-done | bytes 2097168 | tf_op jit(solution)/shard_map/all_gather | solution.py:103
  125.1 5.3 fusion.31
  133.0 2.5 copy.92
  139.0 1.9 fusion.4
  140.9 2.0 fusion.5
  144.1 3.3 divide_convert_fusion
  147.5 4.7 convolution_convert_fusion.3
  152.4 3.2 convert_element_type.184
  155.6 4.6 reshape.552
  160.3 3.7 copy.126
  164.0 5.0 reshape.553
  169.0 62.9 %all_to_all.31 = bf16[8,64,1536]{2,1,0:T(8,128)(2,1)} all-to-all(bf16[8,64,1536]{2,1,0:T(8,128)(2,1)} %reshape.553), channel_id=1, replica_groups=mesh['group'=4,'replica'=8] {'replica'}, dimensions={0} | all-to-all | bytes 3145728 | tf_op jit(solution)/shard_map/all_to_all | solution.py:89
  233.3 2.0 multiply_convert_fusion.3
  235.4 2.4 convert_element_type.186
  238.6 67.4 %all-gather.17.cloned.1.call-done = bf16[2048,1536]{1,0:T(8,128)(2,1)} async-done(((bf16[512,1536]{1,0:T(8,128)(2,1)}), bf16[2048,1536]{1,0:T(8,128)(2,1)}) %all-gather.17.cloned.1.call-update) | async-done | bytes 6291472 | tf_op jit(solution)/shard_map/all_gather | solution.py:103
  306.0 48.9 %all-gather.15.cloned.1.call-done = bf16[1024,2048]{1,0:T(8,128)(2,1)} async-done(((bf16[128,2048]{1,0:T(8,128)(2,1)}), bf16[1024,2048]{1,0:T(8,128)(2,1)}) %all-gather.15.cloned.1.call-update) | async-done | bytes 4194320 | tf_op jit(solution)/shard_map/all_gather | solution.py:79
  354.9 11.8 %fusion.112 = f32[1024,1536]{1,0:T(8,128)} fusion(bf16[1024,2048]{1,0:T(8,128)(2,1)} %all-gather.15.cloned.1.call-done, bf16[2048,1536]{1,0:T(8,128)(2,1)} %all-gather.17.cloned.1.call-done), kind=kOutput, calls=%fused_computation.247 | convolution fusion | flops 6442450944 | bytes 16777216 | tf_op jit(solution)/shard_map/dot_general | solution.py:67
  366.7 33.3 %all-gather.19.cloned.1.call-done = bf16[768,2048]{1,0:T(8,128)(2,1)} async-done(((bf16[192,2048]{1,0:T(8,128)(2,1)}), bf16[768,2048]{1,0:T(8,128)(2,1)}) %all-gather.19.cloned.1.call-update) | async-done | bytes 3145744 | tf_op jit(solution)/shard_map/all_gather | solution.py:103
  400.0 48.5 %all-gather.21.cloned.1.call-done = bf16[1024,2048]{1,0:T(8,128)(2,1)} async-done(((bf16[128,2048]{1,0:T(8,128)(2,1)}), bf16[1024,2048]{1,0:T(8,128)(2,1)}) %all-gather.21.cloned.1.call-update) | async-done | bytes 4194320 | tf_op jit(solution)/shard_map/all_gather | solution.py:79
  448.5 10.5 %multiply_convert_fusion.1 = (bf16[1024,768]{1,0:T(8,128)(2,1)S(1)}, bf16[1024,768]{1,0:T(8,128)(2,1)S(1)}, bf16[1024,768]{1,0:T(8,128)(2,1)}) fusion(f32[1024,1536]{1,0:T(8,128)} %fusion.112, bf16[1024,2048]{1,0:T(8,128)(2,1)} %all-gather.21.cloned.1.call-done, bf16[768,2048]{1,0:T(8,128)(2,1)} %all-gather.19.cloned.1.call-done), kind=kOutput, calls=%fused_computation.35 | convolution fusion | flops 3233021952 | bytes 18350080 | tf_op jit(solution)/shard_map/dot_general | solution.py:71
  460.7 11.0 %convolution_convert_fusion.1 = bf16[1024,2048]{1,0:T(8,128)(2,1)} fusion(bf16[2048,1536]{1,0:T(8,128)(2,1)} %all-gather.17.cloned.1.call-done, bf16[1024,768]{1,0:T(8,128)(2,1)S(1)} %get-tuple-element.50, bf16[1024,768]{1,0:T(8,128)(2,1)S(1)} %get-tuple-element.49), kind=kOutput, calls=%fused_computation.25 | convolution fusion | flops 6450839552 | bytes 13631488 | tf_op jit(solution)/shard_map/dot_general | solution.py:71
  471.8 48.8 %reduce-scatter.15.cloned.1.call-done = bf16[128,2048]{1,0:T(8,128)(2,1)} async-done(((bf16[1024,2048]{1,0:T(8,128)(2,1)}), bf16[128,2048]{1,0:T(8,128)(2,1)}) %reduce-scatter.15.cloned.1.call-update) | async-done | bytes 524304 | tf_op jit(solution)/shard_map/reduce_scatter | solution.py:83
  520.6 1.6 fusion.44
  522.2 2.4 fusion.102
  525.1 11.2 %convolution_convert_fusion = bf16[2048,1536]{1,0:T(8,128)(2,1)} fusion(bf16[1024,2048]{1,0:T(8,128)(2,1)} %all-gather.15.cloned.1.call-done, bf16[1024,768]{1,0:T(8,128)(2,1)} %copy-done.35, bf16[1024,768]{1,0:T(8,128)(2,1)} %copy-done.34), kind=kOutput, calls=%fused_computation.10 | convolution fusion | flops 6451888128 | bytes 13631488 | tf_op jit(solution)/shard_map/dot_general | solution.py:75
  536.4 7.8 convolution_convert_fusion.5
  544.5 25.7 %all-gather.23.cloned.1.call-done = bf16[1024,2048]{1,0:T(8,128)(2,1)} async-done(((bf16[128,2048]{1,0:T(8,128)(2,1)}), bf16[1024,2048]{1,0:T(8,128)(2,1)}) %all-gather.23.cloned.1.call-update) | async-done | bytes 4194320 | tf_op jit(solution)/shard_map/all_gather | solution.py:79
  570.2 4.0 bitcast_reduce_fusion
  574.2 5.3 fusion.10
  579.5 1.8 fusion.23
  582.6 1.6 multiply_reduce_fusion
  584.2 2.5 copy.104
  586.7 1.6 fusion.52
  588.3 4.1 convolution_bitcast_fusion
  594.1 6.5 fusion.36
  600.7 4.3 convolution_convert_fusion.6
  605.1 3.4 convolution_convert_fusion.7
  608.6 17.7 %all_to_all.32 = bf16[4,64,2048]{2,1,0:T(8,128)(2,1)} all-to-all(bf16[4,64,2048]{2,1,0:T(8,128)(2,1)S(1)} %bitcast.253), channel_id=1, replica_groups={{0,1,2,3},{4,5,6,7},{8,9,10,11},{12,13,14,15},{16,17,18,19},{20,21,22,2..., dimensions={0} | all-to-all | bytes 2097152 | tf_op jit(solution)/shard_map/all_to_all | solution.py:98
  626.4 6.0 convolution_convert_fusion.2
  632.4 9.7 %reduce-scatter.21.cloned.1.call-done = bf16[512,1536]{1,0:T(8,128)(2,1)} async-done(((bf16[2048,1536]{1,0:T(8,128)(2,1)}), bf16[512,1536]{1,0:T(8,128)(2,1)}) %reduce-scatter.21.cloned.1.call-update) | async-done | bytes 1572880 | tf_op jit(solution)/shard_map/reduce_scatter | solution.py:106
  642.0 4.6 all-to-all-start.5
  647.4 7.2 convolution_convert_fusion.4
  654.6 34.8 %reduce-scatter.23.cloned.1.call-done = bf16[192,2048]{1,0:T(8,128)(2,1)} async-done(((bf16[768,2048]{1,0:T(8,128)(2,1)}), bf16[192,2048]{1,0:T(8,128)(2,1)}) %reduce-scatter.23.cloned.1.call-update) | async-done | bytes 786448 | tf_op jit(solution)/shard_map/reduce_scatter | solution.py:106
  689.4 5.3 multiply_subtract_fusion.1
  694.7 5.8 reshape.566
  700.5 6.6 copy.125
  707.0 5.3 reshape.565
  712.3 15.8 %reduce-scatter.19.cloned.1.call-done = bf16[512,512]{1,0:T(8,128)(2,1)} async-done(((bf16[2048,512]{1,0:T(8,128)(2,1)}), bf16[512,512]{1,0:T(8,128)(2,1)}) %reduce-scatter.19.cloned.1.call-update) | async-done | bytes 524304 | tf_op jit(solution)/shard_map/reduce_scatter | solution.py:106
  728.1 4.6 all-to-all-start.3
  732.8 8.8 %multiply_subtract_fusion = (f32[64,12288]{1,0:T(8,128)}, f32[64,12288]{1,0:T(8,128)}, f32[64,12288]{1,0:T(8,128)}) fusion(f32[64,12288]{1,0:T(8,128)} %param.31, f32[]{:T(128)} %bitcast.78, f32[]{:T(128)} %bitcast.77, f32[64,12288]{1,0:T(8,128)} %reshape.565, f32[64,12288]{1,0:T(8,128)} %param.33, f32[64,12288]{1,0:T(8,128)} %param.32), kind=kLoop, calls=%fused_computation.32 | loop fusion | flops 11796480 | bytes 22020104 | tf_op jit(solution)/shard_map/sub | solution.py:60
  741.6 17.3 %reduce-scatter.25.cloned.1.call-done = bf16[1,64,2048]{2,1,0:T(8,128)(2,1)} async-done(((bf16[4,64,2048]{2,1,0:T(8,128)(2,1)}), bf16[1,64,2048]{2,1,0:T(8,128)(2,1)}) %reduce-scatter.25.cloned.1.call-update) | async-done | bytes 262160
  758.8 2.4 multiply_subtract_fusion.5
  763.5 2.2 multiply_subtract_fusion.2
  765.7 45.3 %reduce-scatter.17.cloned.1.call-done = bf16[128,2048]{1,0:T(8,128)(2,1)} async-done(((bf16[1024,2048]{1,0:T(8,128)(2,1)}), bf16[128,2048]{1,0:T(8,128)(2,1)}) %reduce-scatter.17.cloned.1.call-update) | async-done | bytes 524304 | tf_op jit(solution)/shard_map/reduce_scatter | solution.py:83
  812.4 39.5 %all-reduce.2 = f32[4352]{0:T(1024)S(1)} all-reduce(f32[4352]{0:T(1024)S(1)} %pad_maximum_fusion.8), channel_id=11, replica_groups=mesh['group'=4,'replica'=8] {'group','replica'}, use_global_device_ids=true, to_apply=%region_26.27.clone | all-reduce | flops 4352 | bytes 34816
  852.7 9.9 %reduce-scatter.13.cloned.1.call-done = bf16[128,2048]{1,0:T(8,128)(2,1)} async-done(((bf16[1024,2048]{1,0:T(8,128)(2,1)}), bf16[128,2048]{1,0:T(8,128)(2,1)}) %reduce-scatter.13.cloned.1.call-update) | async-done | bytes 524304 | tf_op jit(solution)/shard_map/reduce_scatter | solution.py:83
  862.6 3.2 fusion.40
  (186 shorter events, 23.7 us)
Async XLA Ops:
  7.2 82.0 %all-gather.25.cloned.1.call-start = ((), (), s32[]{:S(2)}) async-start(), calls=%async_computation.28 | async-start | bytes 1310720 | tf_op jit(solution)/shard_map/all_gather | solution.py:103
  9.0 24.0 %copy-start.25 = (f32[136]{0:T(256)S(1)}, f32[136]{0:T(256)}, u32[]{:S(2)}) copy-start(f32[136]{0:T(256)} %param.37) | copy-start | bytes 1636
  9.0 24.0 %copy-start.29 = (s32[128]{0:T(128)S(1)}, s32[128]{0:T(128)}, u32[]{:S(2)}) copy-start(s32[128]{0:T(128)} %param.23) | copy-start | bytes 1540
  9.0 75.7 %copy-start.30 = (s32[1,8]{1,0:T(1,128)S(1)}, s32[1,8]{1,0:T(1,128)}, u32[]{:S(2)}) copy-start(s32[1,8]{1,0:T(1,128)} %param.22) | copy-start | bytes 100
  9.0 84.7 %all-gather.11.cloned.1.call-start = ((), (), s32[]{:S(2)}) async-start(), calls=%async_computation.14 | async-start | bytes 4718592 | tf_op jit(solution)/shard_map/all_gather | solution.py:79
  9.8 115.3 %all-gather.13.cloned.1.call-start = ((), (), s32[]{:S(2)}) async-start(), calls=%async_computation.15 | async-start | bytes 2621440 | tf_op jit(solution)/shard_map/all_gather | solution.py:103
  89.2 53.7 %copy-start.4 = (pred[1024,1024]{0,1:T(8,128)(4,1)}, pred[1024,1024]{0,1:T(8,128)(4,1)S(1)}, u32[]{:S(2)}) copy-start(pred[1024,1024]{0,1:T(8,128)(4,1)S(1)} %compare_and_fusion) | copy-start | bytes 3145732
  89.2 58.3 %all-to-all-start.1 = ((bf16[4,64,2048]{2,1,0:T(8,128)(2,1)}), bf16[4,64,2048]{2,1,0:T(8,128)(2,1)}, u32[]{:S(2)}, u32[]{:S(2)}) async-start(bf16[4,64,2048]{2,1,0:T(8,128)(2,1)} %bitcast.252), calls=%async_computation.1 | async-start | bytes 2097152 | tf_op jit(solution)/shard_map/all_to_all | solution.py:98
  93.5 138.5 %reduce-scatter.11.cloned.1.call-start = ((), (), s32[]{:S(2)}) async-start(), calls=%async_computation.16 | async-start | bytes 4718592 | tf_op jit(solution)/shard_map/reduce_scatter | solution.py:83
  139.0 1.9 copy-start.10
  140.9 3.3 copy-start
  152.2 153.8 %all-gather.17.cloned.1.call-start = ((), (), s32[]{:S(2)}) async-start(), calls=%async_computation.18 | async-start | bytes 7864320 | tf_op jit(solution)/shard_map/all_gather | solution.py:103
  169.0 63.0 %copy-start.1 = (bf16[128,2048]{1,0:T(8,128)(2,1)S(1)}, bf16[128,2048]{1,0:T(8,128)(2,1)}, u32[]{:S(2)}) copy-start(bf16[128,2048]{1,0:T(8,128)(2,1)} %param.20) | copy-start | bytes 1572868
  231.9 123.1 %all-gather.15.cloned.1.call-start = ((), (), s32[]{:S(2)}) async-start(), calls=%async_computation.17 | async-start | bytes 4718592 | tf_op jit(solution)/shard_map/all_gather | solution.py:79
  235.3 164.7 %all-gather.19.cloned.1.call-start = ((), (), s32[]{:S(2)}) async-start(), calls=%async_computation.19 | async-start | bytes 3932160 | tf_op jit(solution)/shard_map/all_gather | solution.py:103
  237.8 210.7 %all-gather.21.cloned.1.call-start = ((), (), s32[]{:S(2)}) async-start(), calls=%async_computation.21 | async-start | bytes 4718592 | tf_op jit(solution)/shard_map/all_gather | solution.py:79
  238.6 282.1 %reduce-scatter.15.cloned.1.call-start = ((), (), s32[]{:S(2)}) async-start(), calls=%async_computation.22 | async-start | bytes 4718592 | tf_op jit(solution)/shard_map/reduce_scatter | solution.py:83
  459.0 1.1 copy-start.34
  459.0 1.7 copy-start.35
  471.7 48.9 %copy-start.3 = (bf16[128,2048]{1,0:T(8,128)(2,1)S(1)}, bf16[128,2048]{1,0:T(8,128)(2,1)}, u32[]{:S(2)}) copy-start(bf16[128,2048]{1,0:T(8,128)(2,1)} %reduce-scatter.11.cloned.1.call-done) | copy-start | bytes 1572868
  471.8 98.4 %all-gather.23.cloned.1.call-start = ((), (), s32[]{:S(2)}) async-start(), calls=%async_computation.23 | async-start | bytes 4718592 | tf_op jit(solution)/shard_map/all_gather | solution.py:79
  524.7 117.3 %reduce-scatter.21.cloned.1.call-start = ((), (), s32[]{:S(2)}) async-start(), calls=%async_computation.26 | async-start | bytes 7864320 | tf_op jit(solution)/shard_map/reduce_scatter | solution.py:106
  536.3 153.0 %reduce-scatter.23.cloned.1.call-start = ((), (), s32[]{:S(2)}) async-start(), calls=%async_computation.27 | async-start | bytes 3932160 | tf_op jit(solution)/shard_map/reduce_scatter | solution.py:106
  544.2 183.9 %reduce-scatter.19.cloned.1.call-start = ((), (), s32[]{:S(2)}) async-start(), calls=%async_computation.25 | async-start | bytes 2621440 | tf_op jit(solution)/shard_map/reduce_scatter | solution.py:106
  570.2 4.0 copy-start.5
  574.2 5.3 copy-start.31
  579.5 2.5 copy-start.2
  579.5 1.9 copy-start.12
  579.5 2.0 copy-start.16
  581.3 1.3 copy-start.7
  588.3 12.4 %copy-start.23 = (bf16[1024,256]{0,1:T(8,128)(2,1)}, bf16[1024,256]{0,1:T(8,128)(2,1)S(1)}, u32[]{:S(2)}) copy-start(bf16[1024,256]{0,1:T(8,128)(2,1)S(1)} %get-tuple-element.53) | copy-start | bytes 1572868
  588.3 5.8 copy-start.6
  588.3 5.8 copy-start.32
  594.1 6.6 copy-start.13
  600.7 4.4 copy-start.18
  605.1 153.8 %reduce-scatter.25.cloned.1.call-start = ((), (), s32[]{:S(2)}) async-start(), calls=%async_computation.29 | async-start | bytes 1310720
  608.6 17.8 %copy-start.24 = (bf16[1024,256]{0,1:T(8,128)(2,1)S(1)}, bf16[1024,256]{0,1:T(8,128)(2,1)}, u32[]{:S(2)}) copy-start(bf16[1024,256]{0,1:T(8,128)(2,1)} %copy-done.23) | copy-start | bytes 1572868
  626.3 184.6 %reduce-scatter.17.cloned.1.call-start = ((), (), s32[]{:S(2)}) async-start(), calls=%async_computation.24 | async-start | bytes 4718592 | tf_op jit(solution)/shard_map/reduce_scatter | solution.py:83
  632.3 15.1 %copy-start.33 = (bf16[1024,768]{1,0:T(8,128)(2,1)S(1)}, bf16[1024,768]{1,0:T(8,128)(2,1)}, u32[]{:S(2)}) copy-start(bf16[1024,768]{1,0:T(8,128)(2,1)} %get-tuple-element.51) | copy-start | bytes 4718596
  642.0 52.7 %all-to-all-start.5 = ((bf16[8,64,1536]{2,1,0:T(8,128)(2,1)}), bf16[8,64,1536]{2,1,0:T(8,128)(2,1)}, u32[]{:S(2)}, u32[]{:S(2)}) async-start(bf16[8,64,1536]{2,1,0:T(8,128)(2,1)} %bitcast.249), calls=%async_computation.11 | async-start | bytes 3145728 | tf_op jit(solution)/shard_map/all_to_all | solution.py:89
  646.6 215.9 %reduce-scatter.13.cloned.1.call-start = ((), (), s32[]{:S(2)}) async-start(), calls=%async_computation.20 | async-start | bytes 4718592 | tf_op jit(solution)/shard_map/reduce_scatter | solution.py:83
  654.6 34.8 %copy-start.8 = (f32[192,2048]{1,0:T(8,128)S(1)}, f32[192,2048]{1,0:T(8,128)}, u32[]{:S(2)}) copy-start(f32[192,2048]{1,0:T(8,128)} %param.34) | copy-start | bytes 4718596
  728.1 33.1 %all-to-all-start.3 = ((bf16[8,64,512]{2,1,0:T(8,128)(2,1)}), bf16[8,64,512]{2,1,0:T(8,128)(2,1)S(1)}, u32[]{:S(2)}, u32[]{:S(2)}) async-start(bf16[8,64,512]{2,1,0:T(8,128)(2,1)} %bitcast.254), calls=%async_computation.8 | async-start | bytes 1048576 | tf_op jit(solution)/shard_map/all_to_all | solution.py:89
  732.7 26.1 %copy-start.15 = (f32[64,2048]{1,0:T(8,128)S(1)}, f32[64,2048]{1,0:T(8,128)}, u32[]{:S(2)}) copy-start(f32[64,2048]{1,0:T(8,128)} %param.28) | copy-start | bytes 1572868
  732.7 26.1 %copy-start.21 = (f32[64,2048]{1,0:T(8,128)S(1)}, f32[64,2048]{1,0:T(8,128)}, u32[]{:S(2)}) copy-start(f32[64,2048]{1,0:T(8,128)} %param.30) | copy-start | bytes 1572868
  732.7 26.1 %copy-start.22 = (f32[64,2048]{1,0:T(8,128)S(1)}, f32[64,2048]{1,0:T(8,128)}, u32[]{:S(2)}) copy-start(f32[64,2048]{1,0:T(8,128)} %param.29) | copy-start | bytes 1572868
  761.2 1.6 copy-start.14
  761.2 1.6 copy-start.19
  761.3 2.2 copy-start.20
  761.9 1.0 copy-start.17
  763.5 88.5 %copy-start.26 = (f32[136]{0:T(256)S(1)}, f32[136]{0:T(256)}, u32[]{:S(2)}) copy-start(f32[136]{0:T(256)} %param.37) | copy-start | bytes 1636
  763.5 88.5 %copy-start.27 = (f32[136]{0:T(256)S(1)}, f32[136]{0:T(256)}, u32[]{:S(2)}) copy-start(f32[136]{0:T(256)} %param.39) | copy-start | bytes 1636
  763.5 88.5 %copy-start.28 = (f32[136]{0:T(256)S(1)}, f32[136]{0:T(256)}, u32[]{:S(2)}) copy-start(f32[136]{0:T(256)} %param.38) | copy-start | bytes 1636
  763.5 99.1 %copy-start.9 = (bf16[128,2048]{1,0:T(8,128)(2,1)S(1)}, bf16[128,2048]{1,0:T(8,128)(2,1)}, u32[]{:S(2)}) copy-start(bf16[128,2048]{1,0:T(8,128)(2,1)} %reduce-scatter.15.cloned.1.call-done) | copy-start | bytes 1572868
  763.5 99.1 %copy-start.11 = (bf16[128,2048]{1,0:T(8,128)(2,1)S(1)}, bf16[128,2048]{1,0:T(8,128)(2,1)}, u32[]{:S(2)}) copy-start(bf16[128,2048]{1,0:T(8,128)(2,1)} %param.21) | copy-start | bytes 1572868
Sparse Core Ops, SparseCore 0:
  10.4 29.2 all-gather.24
  41.3 47.9 all-gather.10
  91.1 33.9 all-gather.12
  152.3 70.6 reduce-scatter.10
  232.0 73.9 all-gather.16
  308.0 46.8 all-gather.14
  357.4 42.6 all-gather.18
  401.6 46.8 all-gather.20
  471.9 48.7 reduce-scatter.14
  524.8 45.3 all-gather.22
  573.1 68.8 reduce-scatter.20
  645.4 43.8 reduce-scatter.22
  692.9 35.1 reduce-scatter.18
  730.9 27.9 reduce-scatter.24
  761.0 49.9 reduce-scatter.16
  813.1 49.4 reduce-scatter.12
